TPU v7x, 256 devices: a whole 4x4x8 slice. The times are simulated.
256 devices in a mesh: island: 8 (over y, core), section: 4 (over z_hi), tensor: 8 (over z_lo, x).
Axes of the slice: x: 4, y: 4, z: 8 (z_hi: 4, z_lo: 2; z = z_hi * 2 + z_lo), core: 2. Of those that a mesh axis runs over, the one named last changes fastest.
Arguments:
- hidden: bfloat16 [8, 4, 256, 8192], P('island', 'section', 'tensor'), may hold values from -6 to 6
- norm_gain: bfloat16 [4, 8192], P('section'), may hold values from 0.099609375 to 1.8984375
- grad_above: bfloat16 [8, 256, 8192], P('island', 'tensor'), may hold values from -6 to 6
- key_cot: bfloat16 [8, 4, 256, 1024], P('island', 'section', None, 'tensor'), may hold values from -6 to 6
- value_cot: bfloat16 [8, 4, 256, 1024], P('island', 'section', None, 'tensor'), may hold values from -6 to 6
- local_key: bfloat16 [8, 4, 8192, 1024], P('island', 'section', None, 'tensor'), may hold values from -6 to 6
- local_value: bfloat16 [8, 4, 8192, 1024], P('island', 'section', None, 'tensor'), may hold values from -6 to 6
- anchor_key: float32 [4, 8192, 1024], P('section', 'island', 'tensor'), may hold values from -6 to 6
- anchor_value: float32 [4, 8192, 1024], P('section', 'island', 'tensor'), may hold values from -6 to 6
- momentum_key: float32 [4, 8192, 1024], P('section', 'island', 'tensor'), may hold values from -4 to 4
- momentum_value: float32 [4, 8192, 1024], P('section', 'island', 'tensor'), may hold values from -4 to 4
Outputs:
- anchor_key_new: float32 [4, 8192, 1024], P('section', 'island', 'tensor')
- anchor_value_new: float32 [4, 8192, 1024], P('section', 'island', 'tensor')
- momentum_key_new: float32 [4, 8192, 1024], P('section', 'island', 'tensor')
- momentum_value_new: float32 [4, 8192, 1024], P('section', 'island', 'tensor')
- input_grad: bfloat16 [8, 4, 256, 8192], P('island', 'section', 'tensor')
All inputs are finite; a program needn't handle non-finite values.
Results may differ from a plain program's by a relative error of at most 0.024.
Values may be sent and summed in bfloat16 or wider, within the bound.
A program may use at most 64 MiB of HBM per device.

v0:
```python
import jax
import jax.numpy as jnp
from jax import lax
from jax.sharding import PartitionSpec as P

epsilon = 1e-05
inner_rate = 0.5
outer_rate = 0.7
outer_beta = 0.9


def from_behind(block, axis, distance):
    devices = range(lax.axis_size(axis))
    route = [(i - distance, i) for i in devices if i - distance in devices]
    return lax.ppermute(block, axis, route)


def contract_rows(left, right):
    return lax.dot_general(
        left, right, (((0,), (0,)), ((), ())), preferred_element_type=jnp.float32
    )


def contract_cols(left, right):
    return lax.dot_general(
        left, right, (((1,), (1,)), ((), ())), preferred_element_type=jnp.float32
    )


def outer_update(anchor, momentum, mean_delta):
    momentum_new = outer_beta * momentum + mean_delta
    return (anchor - outer_rate * (mean_delta + outer_beta * momentum_new), momentum_new)


def local(
    hidden,
    norm_gain,
    grad_above,
    key_cot,
    value_cot,
    local_key,
    local_value,
    anchor_key,
    anchor_value,
    momentum_key,
    momentum_value,
):
    resid = hidden[0, 0].astype(jnp.float32)
    gains = norm_gain[0].astype(jnp.float32)
    features = resid.shape[1]
    factor = float(features) ** (-0.5)
    inverse_rms = lax.rsqrt(jnp.mean(resid * resid, axis=-1, keepdims=True) + epsilon)
    normed = (resid * inverse_rms * gains).astype(jnp.bfloat16)
    key_rows = key_cot[0, 0]
    value_rows = value_cot[0, 0]
    weight_key = local_key[0, 0]
    weight_value = local_value[0, 0]
    piece = lax.all_gather(normed, "tensor", axis=0, tiled=True)
    key_piece = key_rows
    value_piece = value_rows
    grad_key = contract_rows(piece, key_piece)
    grad_value = contract_rows(piece, value_piece)
    new_key = weight_key.astype(jnp.float32) - inner_rate * (grad_key * factor)
    new_value = weight_value.astype(jnp.float32) - inner_rate * (grad_value * factor)
    key_piece = key_rows
    value_piece = value_rows
    upstream = lax.psum_scatter(
        (
            (contract_cols(key_piece, weight_key) + contract_cols(value_piece, weight_value))
            * factor
        ).astype(jnp.bfloat16),
        "tensor",
        scatter_dimension=0,
        tiled=True,
    ).astype(jnp.float32)
    scaled = gains * upstream
    branch = inverse_rms * scaled - resid * inverse_rms**3 * jnp.mean(
        resid * scaled, axis=-1, keepdims=True
    )
    is_top = (lax.axis_index("section") == lax.axis_size("section") - 1).astype(jnp.float32)
    own_term = branch + is_top * grad_above[0].astype(jnp.float32)
    running = own_term
    for turn in range(lax.axis_size("section") - 1):
        running = own_term + from_behind(running.astype(jnp.bfloat16), "section", -1).astype(
            running.dtype
        )
    input_grad = running.astype(jnp.bfloat16)[None, None]
    islands = lax.axis_size("island")
    summed_key, summed_value = (
        lax.psum_scatter(
            new_key.astype(jnp.bfloat16), "island", scatter_dimension=0, tiled=True
        ).astype(jnp.float32),
        lax.psum_scatter(
            new_value.astype(jnp.bfloat16), "island", scatter_dimension=0, tiled=True
        ).astype(jnp.float32),
    )
    mean_key = anchor_key[0] - summed_key / islands
    mean_value = anchor_value[0] - summed_value / islands
    anchor_key_new, momentum_key_new = outer_update(anchor_key[0], momentum_key[0], mean_key)
    anchor_value_new, momentum_value_new = outer_update(
        anchor_value[0], momentum_value[0], mean_value
    )
    return (
        anchor_key_new[None],
        anchor_value_new[None],
        momentum_key_new[None],
        momentum_value_new[None],
        input_grad,
    )


def solution(mesh):
    placed = (
        P("island", "section", "tensor", None),
        P("section", None),
        P("island", "tensor", None),
        P("island", "section", None, "tensor"),
        P("island", "section", None, "tensor"),
        P("island", "section", None, "tensor"),
        P("island", "section", None, "tensor"),
        P("section", "island", "tensor"),
        P("section", "island", "tensor"),
        P("section", "island", "tensor"),
        P("section", "island", "tensor"),
    )
    return jax.shard_map(
        local,
        mesh=mesh,
        in_specs=placed,
        out_specs=(
            P("section", "island", "tensor"),
            P("section", "island", "tensor"),
            P("section", "island", "tensor"),
            P("section", "island", "tensor"),
            P("island", "section", "tensor", None),
        ),
        check_vma=False,
    )
```

profile of v0, /device:TPU:1, one launch (start us, length us, event | category | flops | bytes accessed | tf_op | source)
XLA Modules:
  0.0 237.3 jit_solution(14204751072580629089)
XLA Ops:
  7.2 3.0 %fusion.7 = f32[256,8192]{1,0:T(8,128)S(1)} fusion(bf16[1,1,8192,128]{3,2,1,0:T(8,128)(2,1)} %param.16, bf16[1,1,256,128]{3,2,1,0:T(8,128)(2,1)} %param.14), kind=kOutput, calls=%fused_computation.10 | convolution fusion | flops 536870912 | bytes 10551296 | tf_op jit(solution)/shard_map/dot_general | solution.py:25
  10.3 3.2 %fusion.1 = bf16[256,8192]{1,0:T(8,128)(2,1)} fusion(f32[256,8192]{1,0:T(8,128)S(1)} %fusion.7, bf16[1,1,8192,128]{3,2,1,0:T(8,128)(2,1)S(1)} %copy-done.1, bf16[1,1,256,128]{3,2,1,0:T(8,128)(2,1)S(1)} %copy-done), kind=kOutput, calls=%fused_computation.2 | convolution fusion | flops 543162368 | bytes 14745600 | tf_op jit(solution)/shard_map/dot_general | solution.py:25
  13.6 0.0 all-gather.2.cloned.1.call-start
  13.6 0.7 copy-done.9
  14.3 58.8 %reduce-scatter.8.cloned.1.call-done = bf16[32,8192]{1,0:T(8,128)(2,1)} async-done(((bf16[256,8192]{1,0:T(8,128)(2,1)}), bf16[32,8192]{1,0:T(8,128)(2,1)}) %reduce-scatter.8.cloned.1.call-update) | async-done | bytes 524304 | tf_op jit(solution)/shard_map/reduce_scatter | solution.py:67
  73.1 1.4 fusion.15
  74.5 2.8 %fusion.25 = (bf16[32,8192]{1,0:T(8,128)(2,1)}, f32[32,8192]{1,0:T(8,128)S(1)}, bf16[32,8192]{1,0:T(8,128)(2,1)}) fusion(bf16[1,32,8192]{2,1,0:T(8,128)(2,1)} %param.13, f32[]{:T(128)S(6)} %convert_element_type.74, f32[32]{0:T(128)S(1)} %get-tuple-element.16, f32[32]{0:T(128)S(1)} %get-tuple-element.14, bf16[1,1,32,8192]{3,2,1,0:T(8,128)(2,1)} %param.11, ...), kind=kLoop, calls=%fused_computation.45 | loop fusion | flops 3670016 | bytes 3703172 | tf_op jit(solution)/shard_map/convert_element_type | solution.py:84
  77.4 0.0 reduce-scatter.6.cloned.1.call-start
  77.4 53.9 %all-gather.2.cloned.1.call-done = bf16[256,8192]{1,0:T(8,128)(2,1)} async-done(((bf16[32,8192]{1,0:T(8,128)(2,1)}), bf16[256,8192]{1,0:T(8,128)(2,1)}) %all-gather.2.cloned.1.call-update) | async-done | bytes 4194320 | tf_op jit(solution)/shard_map/all_gather | solution.py:58
  131.4 4.8 %fusion.5 = bf16[8192,128]{1,0:T(8,128)(2,1)} fusion(bf16[256,8192]{1,0:T(8,128)(2,1)} %all-gather.2.cloned.1.call-done, bf16[1,1,8192,128]{3,2,1,0:T(8,128)(2,1)S(1)} %copy-done.1, bf16[1,1,256,128]{3,2,1,0:T(8,128)(2,1)S(1)} %copy-done), kind=kOutput, calls=%fused_computation.8 | convolution fusion | flops 541065216 | bytes 8454144 | tf_op jit(solution)/shard_map/dot_general | solution.py:19
  136.2 0.0 reduce-scatter.4.cloned.1.call-start
  136.3 1.4 collective-permute-start
  137.7 37.9 %collective-permute-done = bf16[32,8192]{1,0:T(8,128)(2,1)S(1)} collective-permute-done((bf16[32,8192]{1,0:T(8,128)(2,1)}, bf16[32,8192]{1,0:T(8,128)(2,1)S(1)}, u32[]{:S(2)}, u32[]{:S(2)}) %collective-permute-start) | collective-permute-done | bytes 524320 | tf_op jit(solution)/shard_map/ppermute | solution.py:15
  175.7 0.9 add_convert_fusion.2
  176.5 1.3 collective-permute-start.1
  177.8 4.8 %fusion.4 = bf16[8192,128]{1,0:T(8,128)(2,1)} fusion(bf16[256,8192]{1,0:T(8,128)(2,1)} %all-gather.2.cloned.1.call-done, bf16[1,1,8192,128]{3,2,1,0:T(8,128)(2,1)S(1)} %copy-done.2, bf16[1,1,256,128]{3,2,1,0:T(8,128)(2,1)S(1)} %copy-done.8), kind=kOutput, calls=%fused_computation.7 | convolution fusion | flops 541065216 | bytes 8454144 | tf_op jit(solution)/shard_map/dot_general | solution.py:19
  182.7 21.7 %collective-permute-done.1 = bf16[32,8192]{1,0:T(8,128)(2,1)} collective-permute-done((bf16[32,8192]{1,0:T(8,128)(2,1)}, bf16[32,8192]{1,0:T(8,128)(2,1)}, u32[]{:S(2)}, u32[]{:S(2)}) %collective-permute-start.1) | collective-permute-done | bytes 524320 | tf_op jit(solution)/shard_map/ppermute | solution.py:15
  204.4 1.1 add_convert_fusion.1
  205.6 1.3 collective-permute-start.2
  206.9 14.5 %collective-permute-done.2 = bf16[32,8192]{1,0:T(8,128)(2,1)S(1)} collective-permute-done((bf16[32,8192]{1,0:T(8,128)(2,1)S(1)}, bf16[32,8192]{1,0:T(8,128)(2,1)S(1)}, u32[]{:S(2)}, u32[]{:S(2)}) %collective-permute-start.2) | collective-permute-done | bytes 524320 | tf_op jit(solution)/shard_map/ppermute | solution.py:15
  221.4 0.9 fusion.16
  222.3 2.1 fusion.20
  224.3 4.3 %reduce-scatter.4.cloned.1.call-done = bf16[1024,128]{1,0:T(8,128)(2,1)} async-done(((bf16[8192,128]{1,0:T(8,128)(2,1)}), bf16[1024,128]{1,0:T(8,128)(2,1)}) %reduce-scatter.4.cloned.1.call-update) | async-done | bytes 262160 | tf_op jit(solution)/shard_map/reduce_scatter | solution.py:90
  228.7 2.1 fusion.19
  (27 shorter events, 0.2 us)
Async XLA Ops:
  7.2 3.1 %copy-start = (bf16[1,1,256,128]{3,2,1,0:T(8,128)(2,1)S(1)}, bf16[1,1,256,128]{3,2,1,0:T(8,128)(2,1)}, u32[]{:S(2)}) copy-start(bf16[1,1,256,128]{3,2,1,0:T(8,128)(2,1)} %param.15) | copy-start | bytes 196612
  7.2 3.1 %copy-start.1 = (bf16[1,1,8192,128]{3,2,1,0:T(8,128)(2,1)S(1)}, bf16[1,1,8192,128]{3,2,1,0:T(8,128)(2,1)}, u32[]{:S(2)}) copy-start(bf16[1,1,8192,128]{3,2,1,0:T(8,128)(2,1)} %param.17) | copy-start | bytes 6291460
  7.2 65.9 %reduce-scatter.8.cloned.1.call-start = ((), (), s32[]{:S(2)}) async-start(), calls=%async_computation.6 | async-start | bytes 4718592 | tf_op jit(solution)/shard_map/reduce_scatter | solution.py:67
  13.5 0.8 copy-start.9
  13.5 59.6 %copy-start.3 = (bf16[1,1,32,8192]{3,2,1,0:T(8,128)(2,1)S(1)}, bf16[1,1,32,8192]{3,2,1,0:T(8,128)(2,1)}, u32[]{:S(2)}) copy-start(bf16[1,1,32,8192]{3,2,1,0:T(8,128)(2,1)} %param.11) | copy-start | bytes 1572868
  13.6 117.8 %all-gather.2.cloned.1.call-start = ((), (), s32[]{:S(2)}) async-start(), calls=%async_computation.3 | async-start | bytes 4718592 | tf_op jit(solution)/shard_map/all_gather | solution.py:58
  77.4 144.9 %reduce-scatter.6.cloned.1.call-start = ((), (), s32[]{:S(2)}) async-start(), calls=%async_computation.5 | async-start | bytes 2359296 | tf_op jit(solution)/shard_map/reduce_scatter | solution.py:93
  136.2 41.6 %copy-start.2 = (bf16[1,1,8192,128]{3,2,1,0:T(8,128)(2,1)S(1)}, bf16[1,1,8192,128]{3,2,1,0:T(8,128)(2,1)}, u32[]{:S(2)}) copy-start(bf16[1,1,8192,128]{3,2,1,0:T(8,128)(2,1)} %param.16) | copy-start | bytes 6291460
  136.2 41.6 %copy-start.8 = (bf16[1,1,256,128]{3,2,1,0:T(8,128)(2,1)S(1)}, bf16[1,1,256,128]{3,2,1,0:T(8,128)(2,1)}, u32[]{:S(2)}) copy-start(bf16[1,1,256,128]{3,2,1,0:T(8,128)(2,1)} %param.14) | copy-start | bytes 196612
  136.2 92.4 %reduce-scatter.4.cloned.1.call-start = ((), (), s32[]{:S(2)}) async-start(), calls=%async_computation.4 | async-start | bytes 2359296 | tf_op jit(solution)/shard_map/reduce_scatter | solution.py:90
  136.3 39.4 %collective-permute-start = (bf16[32,8192]{1,0:T(8,128)(2,1)}, bf16[32,8192]{1,0:T(8,128)(2,1)S(1)}, u32[]{:S(2)}, u32[]{:S(2)}) collective-permute-start(bf16[32,8192]{1,0:T(8,128)(2,1)} %get-tuple-element.7), channel_id=1, source_target_pairs={{8,0},{16,8},{24,16},{9,1},{17,9},{25,17},{10,2},{18,10},{26,18},{... | collective-permute-start | bytes 1572872 | tf_op jit(solution)/shard_map/ppermute | solution.py:15
  176.5 27.9 %collective-permute-start.1 = (bf16[32,8192]{1,0:T(8,128)(2,1)}, bf16[32,8192]{1,0:T(8,128)(2,1)}, u32[]{:S(2)}, u32[]{:S(2)}) collective-permute-start(bf16[32,8192]{1,0:T(8,128)(2,1)} %add_convert_fusion.2), channel_id=1, source_target_pairs={{8,0},{16,8},{24,16},{9,1},{17,9},{25,17},{10,2},{18,10},{26,18},{... | collective-permute-start | bytes 1572872 | tf_op jit(solution)/shard_map/ppermute | solution.py:15
  182.7 39.6 %copy-start.4 = (f32[1,1024,128]{2,1,0:T(8,128)S(1)}, f32[1,1024,128]{2,1,0:T(8,128)}, u32[]{:S(2)}) copy-start(f32[1,1024,128]{2,1,0:T(8,128)} %param.19) | copy-start | bytes 1572868
  182.7 39.6 %copy-start.5 = (f32[1,1024,128]{2,1,0:T(8,128)S(1)}, f32[1,1024,128]{2,1,0:T(8,128)}, u32[]{:S(2)}) copy-start(f32[1,1024,128]{2,1,0:T(8,128)} %param.21) | copy-start | bytes 1572868
  182.7 46.0 %copy-start.6 = (f32[1,1024,128]{2,1,0:T(8,128)S(1)}, f32[1,1024,128]{2,1,0:T(8,128)}, u32[]{:S(2)}) copy-start(f32[1,1024,128]{2,1,0:T(8,128)} %param.18) | copy-start | bytes 1572868
  182.7 46.0 %copy-start.7 = (f32[1,1024,128]{2,1,0:T(8,128)S(1)}, f32[1,1024,128]{2,1,0:T(8,128)}, u32[]{:S(2)}) copy-start(f32[1,1024,128]{2,1,0:T(8,128)} %param.20) | copy-start | bytes 1572868
  205.6 15.8 %collective-permute-start.2 = (bf16[32,8192]{1,0:T(8,128)(2,1)S(1)}, bf16[32,8192]{1,0:T(8,128)(2,1)S(1)}, u32[]{:S(2)}, u32[]{:S(2)}) collective-permute-start(bf16[32,8192]{1,0:T(8,128)(2,1)S(1)} %add_convert_fusion.1), channel_id=1, source_target_pairs={{8,0},{16,8},{24,16},{9,1},{17,9},{25,17},{10,2},{18,10},{26,18},{... | collective-permute-start | bytes 1572872 | tf_op jit(solution)/shard_map/ppermute | solution.py:15
Sparse Core Ops, SparseCore 0:
  13.7 59.4 reduce-scatter.7
  77.5 53.8 all-gather.1
  136.4 32.9 reduce-scatter.5
  182.8 45.7 reduce-scatter.3
where the time goes:
time: 239 us; the launch traced here: 237 us
  waiting for transfers between devices  191 us (80%)
  matrix products  16 us (7%)
  between operations  13.9 us (6%)
  other arithmetic  11.3 us (5%)
  starting transfers between devices  4.16 us (2%)
    ppermute x3, waiting for transfers between devices, from_behind(): return lax.ppermute(block, axis, route)  74.1 us
    reduce_scatter x1, waiting for transfers between devices, local(): lax.psum_scatter(((contract_cols(key_piece, weight_key) + contract_cols(v...  58.8 us
    all_gather x1, waiting for transfers between devices, local(): piece = lax.all_gather(normed, 'tensor', axis=0, tiled=True)  53.9 us
    dot_general x2, matrix products, contract_rows(): lax.dot_general(left, right, (((0,), (0,)), ((), ())), preferred_element_...  9.69 us
    dot_general x2, matrix products, contract_cols(): lax.dot_general(left, right, (((1,), (1,)), ((), ())), preferred_element_...  6.27 us
    convert_element_type x3, other arithmetic, local(): running.astype(jnp.bfloat16)  4.83 us
  transfers between devices with their start and end apart: 7, of which 6 were waited for; matrix products, arithmetic and copies ran while one was open for 4% of the time, Pallas kernels for 0%

commit v1 on v0

v1 whole, which is shorter than its diff:
```python
import types

import jax
import jax.numpy as jnp
from jax import lax
from jax.experimental import pallas as pl
from jax.experimental.pallas import tpu as pltpu
from jax.sharding import PartitionSpec as P

MESH = pl.DeviceIdType.MESH
BF = jnp.bfloat16
F32 = jnp.float32

epsilon = 1e-05
inner_rate = 0.5
outer_rate = 0.7
outer_beta = 0.9

D = 8192
TOK = 256
NX, NY, NZ, NS = 4, 4, 2, 4
HALF = D // 2
STEP = 512
NSTEP = D // STEP
PIECES = 4
PIECE = D // PIECES
FACTOR = float(D) ** (-0.5)

SCRATCH = dict(
    hid=((32, D), BF),
    gain=((1, D), BF),
    above=((32, D), BF),
    cot=((TOK, 256), BF),
    w=((4, 4, 512, 256), BF),
    anc=((2, 1024, 128), F32),
    mom=((2, 1024, 128), F32),
    inv=((32, 128), F32),
    p=((8, 2, 16, D), BF),
    xo=((2, 2, 16, D), BF),
    r1=((2, 2, 16, HALF), BF),
    xw=((2, 2, 16, D), BF),
    z1=((2, 16, D), BF),
    z2=((2, 16, D), BF),
    z2s=((2, 16, D), BF),
    scaled=((2, 16, D), F32),
    coef=((2, 16, 128), F32),
    ch=((2, 16, D), BF),
    chs=((2, 16, D), BF),
    wc=((4, 2, 512, 256), BF),
    w1=((2, 512, 256), BF),
    wy=((2, 2, 512, 256), BF),
    na=((8, 32, 1024), BF),
    ar=((8, 32, 1024), BF),
    at=((4, 2, 512, 256), BF),
    cb=((4, 2, 32, 256), BF),
    bz=((4, 2, 32, 256), BF),
    b=((4, 2, 4, 2, 32, 256), BF),
    gcs=((2, 512, 256), BF),
    gc=((2, 512, 256), BF),
    gzs=((2, 256, 256), BF),
    gz=((2, 256, 256), BF),
    own=((512, 256), F32),
)
NREMOTE = 80
NLOCAL = 16


def contract_cols(left, right):
    return lax.dot_general(left, right, (((1,), (1,)), ((), ())), preferred_element_type=F32)


def contract(left, right):
    return lax.dot_general(left, right, (((1,), (0,)), ((), ())), preferred_element_type=F32)


def lanes(v):
    total = v[:, 0:128]
    for k in range(1, v.shape[1] // 128):
        total = total + v[:, 128 * k : 128 * (k + 1)]
    return total


def at_step(q, width=STEP):
    return pl.ds(pl.multiple_of(q * width, width), width)


def loop(n, body):
    def step(q, carry):
        body(q)
        return carry

    lax.fori_loop(0, n, step, 0)


def kernel(*refs):
    (hid_h, gain_h, above_h, kc_h, vc_h, wk_h, wv_h, ak_h, av_h, mk_h, mv_h) = refs[:11]
    o_ak, o_av, o_mk, o_mv, o_ig = refs[11:16]
    s = types.SimpleNamespace(**dict(zip(SCRATCH, refs[16 : 16 + len(SCRATCH)])))
    ssem, rsem, lsem = refs[16 + len(SCRATCH) :]

    island = lax.axis_index("island")
    sec = lax.axis_index("section")
    tensor = lax.axis_index("tensor")
    y, c = island // 2, lax.rem(island, 2)
    zl, x = tensor // 4, lax.rem(tensor, 4)
    oz, oc = 1 - zl, 1 - c
    slot = y * 2 + zl

    def xdev(d):
        return {"tensor": zl * 4 + lax.rem(x + d + 4, 4)}

    def ydev(d):
        return {"island": lax.rem(y + d + 4, 4) * 2 + c}

    zdev = {"tensor": oz * 4 + x}
    cdev = {"island": y * 2 + oc}

    def slotdev(k):
        return {"island": (k // 2) * 2 + c, "tensor": lax.rem(k, 2) * 4 + x}

    count = [0]
    sent = []

    def remote(src, dst, dev, keep=True):
        k = count[0]
        count[0] += 1
        copy = pltpu.make_async_remote_copy(
            src_ref=src,
            dst_ref=dst,
            send_sem=ssem.at[k],
            recv_sem=rsem.at[k],
            device_id=dev,
            device_id_type=MESH,
        )
        if keep:
            sent.append(copy)
        return copy

    nload = [0]

    def load(src, dst):
        copy = pltpu.make_async_copy(src, dst, lsem.at[nload[0]])
        nload[0] += 1
        copy.start()
        return copy

    lw = [
        load(wk_h, s.w.at[:, :, :, pl.ds(0, 128)]),
        load(wv_h, s.w.at[:, :, :, pl.ds(128, 128)]),
    ]
    lc = [load(kc_h, s.cot.at[:, pl.ds(0, 128)]), load(vc_h, s.cot.at[:, pl.ds(128, 128)])]
    lh = [load(hid_h, s.hid), load(gain_h, s.gain)]
    late = [
        load(above_h, s.above),
        load(ak_h, s.anc.at[0]),
        load(av_h, s.anc.at[1]),
        load(mk_h, s.mom.at[0]),
        load(mv_h, s.mom.at[1]),
    ]

    barrier = pltpu.get_barrier_semaphore()
    partners = [cdev, xdev(1), xdev(-1)]
    partners += [slotdev(lax.rem(slot + d, 8)) for d in range(1, 8)]
    partners += [{"section": lax.rem(sec + 1, NS)}, {"section": lax.rem(sec + 3, NS)}]
    for dev in partners:
        pl.semaphore_signal(barrier, inc=1, device_id=dev, device_id_type=MESH)

    @pl.when(sec == NS - 1)
    def _():
        def zero(q):
            s.ch[:, :, at_step(q)] = jnp.zeros((2, 16, STEP), BF)

        loop(NSTEP, zero)

    for copy in lc:
        copy.wait()
    for xx in range(4):
        for zz in range(2):
            t = (zz * 4 + xx) * 32
            s.cb[xx, zz] = s.cot[t : t + 32, :]
    pl.semaphore_wait(barrier, len(partners))

    bzc = remote(s.cb, s.bz, zdev)
    bzc.start()

    for copy in lw:
        copy.wait()
    wcc = remote(s.w.at[:, pl.ds(oc * 2, 2)], s.wc, cdev)
    wcc.start()

    def partial(q):
        val = contract_cols(s.cot[...], s.w[q // 4, lax.rem(q, 4)]) * FACTOR
        fs = at_step(q)
        for r in range(16):
            s.p[r // 2, r % 2, :, fs] = val[16 * r : 16 * r + 16].astype(BF)

    loop(NSTEP, partial)

    fa, fb = pl.ds(0, HALF), pl.ds(HALF, HALF)
    x_r, x_l, x_2 = lax.rem(x + 1, 4), lax.rem(x + 3, 4), lax.rem(x + 2, 4)

    z1c = [remote(s.p.at[oz * 4 + x_2, h], s.z1.at[h], zdev) for h in range(2)]
    xoc = [
        [
            remote(s.p.at[oz * 4 + x_r, h], s.xo.at[0, h], xdev(1)),
            remote(s.p.at[oz * 4 + x_l, h], s.xo.at[1, h], xdev(-1)),
        ]
        for h in range(2)
    ]
    nac = [
        [
            remote(s.p.at[zl * 4 + x_r, h, :, fb], s.xw.at[0, h, :, fb], xdev(1)),
            remote(s.p.at[zl * 4 + x_l, h, :, fa], s.xw.at[1, h, :, fa], xdev(-1)),
        ]
        for h in range(2)
    ]
    r1c = [
        [
            remote(s.p.at[zl * 4 + x_2, h, :, fa], s.r1.at[0, h], xdev(1)),
            remote(s.p.at[zl * 4 + x_2, h, :, fb], s.r1.at[1, h], xdev(-1)),
        ]
        for h in range(2)
    ]
    agc = [
        [
            remote(s.p.at[zl * 4 + x_r, h, :, fa], s.xw.at[0, h, :, fa], xdev(1)),
            remote(s.p.at[zl * 4 + x_l, h, :, fb], s.xw.at[1, h, :, fb], xdev(-1)),
        ]
        for h in range(2)
    ]
    z2c = [remote(s.z2s.at[h], s.z2.at[h], zdev) for h in range(2)]

    def start_direct(h):
        for copy in xoc[h] + nac[h]:
            copy.start()

    def far_block(h):
        z1c[h].wait_recv()

        def add(q):
            fs = at_step(q)
            s.p[zl * 4 + x_2, h, :, fs] = (
                s.p[zl * 4 + x_2, h, :, fs].astype(F32) + s.z1[h, :, fs].astype(F32)
            ).astype(BF)

        loop(NSTEP, add)
        for copy in r1c[h]:
            copy.start()

    def aggregate(h):
        for d, (xi, off) in enumerate(((x_r, 0), (x_l, HALF))):
            r1c[h][d].wait_recv()

            def add(q):
                src = pl.ds(pl.multiple_of(q * STEP, STEP), STEP)
                fs = pl.ds(pl.multiple_of(off + q * STEP, STEP), STEP)
                s.p[zl * 4 + xi, h, :, fs] = (
                    s.p[zl * 4 + xi, h, :, fs].astype(F32) + s.r1[d, h, :, src].astype(F32)
                ).astype(BF)

            loop(NSTEP // 2, add)
            agc[h][d].start()

    def send_across(h):
        for copy in xoc[h]:
            copy.wait_recv()

        def add(q):
            fs = at_step(q)
            s.z2s[h, :, fs] = (
                s.p[oz * 4 + x, h, :, fs].astype(F32)
                + s.xo[0, h, :, fs].astype(F32)
                + s.xo[1, h, :, fs].astype(F32)
            ).astype(BF)

        loop(NSTEP, add)
        z2c[h].start()

    z1c[0].start()
    start_direct(0)
    z1c[1].start()

    for copy in lh:
        copy.wait()

    def square(q, acc):
        seg = s.hid[:, at_step(q)].astype(F32)
        return acc + lanes(seg * seg)

    squares = lax.fori_loop(0, NSTEP, square, jnp.zeros((32, 128), F32))
    inverse = lax.rsqrt(jnp.sum(squares, axis=1, keepdims=True) / D + epsilon)
    s.inv[...] = jnp.broadcast_to(inverse, (32, 128))

    def norm(q):
        fs = at_step(q)
        inv = s.inv[:, 0:1]
        val = s.hid[:, fs].astype(F32) * inv * s.gain[:, fs].astype(F32)
        lane = pl.ds(pl.multiple_of(lax.rem(q // 2, 2) * STEP, STEP), STEP)
        s.na[(q // 4) * 2 + lax.rem(q, 2), :, lane] = val.astype(BF)

    loop(NSTEP, norm)
    ac = []
    for d in range(1, 8):
        k = lax.rem(slot + d, 8)
        copy = remote(s.na.at[k], s.ar.at[slot], slotdev(k))
        copy.start()
        ac.append(copy)
    s.ar[slot] = s.na[slot]

    bc = []
    for d in range(1, 4):
        copy = remote(s.cb, s.b.at[y, zl], ydev(d))
        copy.start()
        bc.append(copy)
    s.b[y, zl] = s.cb[...]
    bzc.wait_recv()
    for d in range(1, 4):
        copy = remote(s.bz, s.b.at[y, oz], ydev(d))
        copy.start()
        bc.append(copy)
    s.b[y, oz] = s.bz[...]

    far_block(0)

    wcc.wait_recv()

    def pair(q):
        yy, hh = q // 4, lax.rem(q // 2, 2)
        rows = pl.ds(pl.multiple_of(lax.rem(q, 2) * 256, 256), 256)
        s.w[yy, c * 2 + hh, rows, :] = (
            s.w[yy, c * 2 + hh, rows, :].astype(F32) + s.wc[yy, hh, rows, :].astype(F32)
        ).astype(BF)

    loop(16, pair)
    y_r, y_l, y_2 = lax.rem(y + 1, 4), lax.rem(y + 3, 4), lax.rem(y + 2, 4)
    w1c = [
        remote(s.w.at[y_2, c * 2], s.w1.at[0], ydev(1)),
        remote(s.w.at[y_2, c * 2 + 1], s.w1.at[1], ydev(-1)),
    ]
    wnc = [
        remote(s.w.at[y_r, c * 2 + 1], s.wy.at[0, 1], ydev(1)),
        remote(s.w.at[y_l, c * 2], s.wy.at[1, 0], ydev(-1)),
    ]
    wac = [
        remote(s.w.at[y_r, c * 2], s.wy.at[0, 0], ydev(1)),
        remote(s.w.at[y_l, c * 2 + 1], s.wy.at[1, 1], ydev(-1)),
    ]
    for copy in w1c + wnc:
        copy.start()

    aggregate(0)
    start_direct(1)
    far_block(1)

    for copy in ac:
        copy.wait_recv()

    def turn(q):
        fs = pl.ds(pl.multiple_of(q * 128, 128), 128)
        block = s.ar[:, :, fs].reshape(TOK, 128)
        rows = pl.ds(pl.multiple_of(lax.rem(q, 4) * 128, 128), 128)
        s.at[x, q // 4, rows, :] = block.T

    loop(8, turn)

    send_across(0)
    aggregate(1)

    ra, rb = pl.ds(0, 256), pl.ds(256, 256)
    gat = []
    rel = []
    for cc in (oc, c):
        gat.append(
            [
                [remote(s.at.at[x, cc, part], s.at.at[x, cc, part], xdev(1)) for part in (ra, rb)],
                [remote(s.at.at[x, cc, part], s.at.at[x, cc, part], xdev(-1)) for part in (rb, ra)],
            ]
        )
        rel.append(
            [
                remote(s.at.at[x_l, cc, ra], s.at.at[x_l, cc, ra], xdev(1)),
                remote(s.at.at[x_r, cc, rb], s.at.at[x_r, cc, rb], xdev(-1)),
            ]
        )

    def start_gather(f):
        for k in range(2):
            for d in range(2):
                gat[f][d][k].start()

    def relay(f):
        for d in range(2):
            gat[f][d][0].wait_recv()
            rel[f][d].start()

    start_gather(0)

    for d, yi in enumerate((y_r, y_l)):
        w1c[d].wait_recv()

        def add(q, d=d, yi=yi):
            rows = pl.ds(pl.multiple_of(q * 128, 128), 128)
            s.w[yi, c * 2 + d, rows, :] = (
                s.w[yi, c * 2 + d, rows, :].astype(F32) + s.w1[d, rows, :].astype(F32)
            ).astype(BF)

        loop(4, add)
        wac[d].start()

    for copy in late:
        copy.wait()

    def branch(h):
        for d in range(2):
            nac[h][d].wait_recv()
            agc[h][d].wait_recv()
        z2c[h].wait_recv()
        rows = pl.ds(h * 16, 16)

        def first(q, acc):
            fs = at_step(q)
            up = (
                s.p[zl * 4 + x, h, :, fs].astype(F32)
                + s.xw[0, h, :, fs].astype(F32)
                + s.xw[1, h, :, fs].astype(F32)
                + s.z2[h, :, fs].astype(F32)
            )
            scaled = s.gain[:, fs].astype(F32) * up
            s.scaled[h, :, fs] = scaled
            return acc + lanes(s.hid[rows, fs].astype(F32) * scaled)

        dots = lax.fori_loop(0, NSTEP, first, jnp.zeros((16, 128), F32))
        mean = jnp.sum(dots, axis=1, keepdims=True) / D
        inv = s.inv[rows, 0:1]
        s.coef[h] = jnp.broadcast_to(inv * inv * inv * mean, (16, 128))

    chc = [
        [
            remote(
                s.chs.at[h, :, pl.ds(k * PIECE, PIECE)],
                s.ch.at[h, :, pl.ds(k * PIECE, PIECE)],
                {"section": lax.rem(sec + 3, NS)},
                keep=False,
            )
            for k in range(PIECES)
        ]
        for h in range(2)
    ]

    def chain(h):
        rows = pl.ds(h * 16, 16)
        for k in range(PIECES):

            @pl.when(sec < NS - 1)
            def _():
                chc[h][k].wait_recv()

            inv = s.inv[rows, 0:1]
            coef = s.coef[h, :, 0:1]

            def run(q):
                fs = pl.ds(pl.multiple_of(k * PIECE + q * STEP, STEP), STEP)
                term = inv * s.scaled[h, :, fs] - s.hid[rows, fs].astype(F32) * coef
                term = term + s.ch[h, :, fs].astype(F32)
                s.chs[h, :, fs] = term.astype(BF)
                o_ig[rows, fs] = (term + s.above[rows, fs].astype(F32)).astype(BF)

            loop(PIECE // STEP, run)

            @pl.when(sec > 0)
            def _():
                chc[h][k].start()

    branch(0)

    @pl.when(sec >= 2)
    def _():
        chain(0)

    send_across(1)
    start_gather(1)
    relay(0)

    @pl.when(sec == 1)
    def _():
        chain(0)

    branch(1)

    @pl.when(sec == 3)
    def _():
        chain(1)

    @pl.when(sec == 0)
    def _():
        chain(0)

    relay(1)

    def products(cc, zc, rows):
        total = None
        for xx in range(4):
            left = s.at[xx, cc, rows, :]
            right = s.b[:, zc, xx].reshape(256, 256)
            part = contract(left, right)
            total = part if total is None else total + part
        return total

    for copy in bc:
        copy.wait_recv()

    def arrived(f):
        for d in range(2):
            gat[f][d][1].wait_recv()
            rel[f][d].wait_recv()

    blocks = [pl.ds(0, 256), pl.ds(256, 256)]
    arrived(0)
    gcc = remote(s.gcs, s.gc, cdev)

    def other_core(q):
        rows = pl.ds(pl.multiple_of(lax.rem(q, 2) * 256, 256), 256)
        s.gcs[q // 2, rows, :] = products(oc, q // 2, rows).astype(BF)

    loop(4, other_core)
    gcc.start()

    @pl.when(sec == 2)
    def _():
        chain(1)

    arrived(1)
    gcc.wait_recv()
    gzc = []
    for k, rows in enumerate(blocks):
        s.gzs[k] = (products(c, oz, rows) + s.gc[oz, rows, :].astype(F32)).astype(BF)
        copy = remote(s.gzs.at[k], s.gz.at[k], zdev)
        copy.start()
        gzc.append(copy)
    for rows in blocks:
        s.own[rows, :] = products(c, zl, rows) + s.gc[zl, rows, :].astype(F32)

    @pl.when(sec <= 1)
    def _():
        chain(1)

    for copy in wnc + wac:
        copy.wait_recv()

    def finish(half, rows, base, grad):
        for kv, (oa, om) in enumerate(((o_ak, o_mk), (o_av, o_mv))):
            cols = pl.ds(kv * 128, 128)
            out = pl.ds(pl.multiple_of(half * 512 + base, 128), 128)
            total = (
                s.w[y, c * 2 + half, rows, cols].astype(F32)
                + s.wy[0, half, rows, cols].astype(F32)
                + s.wy[1, half, rows, cols].astype(F32)
            )
            total = total - (inner_rate * FACTOR) * grad[:, kv * 128 : kv * 128 + 128]
            anchor = s.anc[kv, out, :]
            mean = anchor - total * 0.125
            moment = outer_beta * s.mom[kv, out, :] + mean
            om[out, :] = moment
            oa[out, :] = anchor - outer_rate * (mean + outer_beta * moment)

    def finish_own(q):
        rows = pl.ds(pl.multiple_of(q * 128, 128), 128)
        finish(zl, rows, q * 128, s.own[rows, :])

    loop(4, finish_own)
    for copy in gzc:
        copy.wait_recv()

    def finish_other(q):
        rows = pl.ds(pl.multiple_of(q * 128, 128), 128)
        inner = pl.ds(pl.multiple_of(lax.rem(q, 2) * 128, 128), 128)
        finish(oz, rows, q * 128, s.gz[q // 2, inner, :].astype(F32))

    loop(4, finish_other)

    for copy in sent:
        copy.wait_send()

    @pl.when(sec > 0)
    def _():
        for h in range(2):
            for copy in chc[h]:
                copy.wait_send()


def local(hidden, gain, above, kc, vc, wk, wv, ak, av, mk, mv):
    outs = pl.pallas_call(
        kernel,
        out_shape=[jax.ShapeDtypeStruct((1024, 128), F32)] * 4
        + [jax.ShapeDtypeStruct((32, D), BF)],
        in_specs=[pl.BlockSpec(memory_space=pl.ANY)] * 11,
        out_specs=[pl.BlockSpec(memory_space=pltpu.VMEM)] * 5,
        scratch_shapes=[pltpu.VMEM(shape, kind) for shape, kind in SCRATCH.values()]
        + [
            pltpu.SemaphoreType.DMA((NREMOTE,)),
            pltpu.SemaphoreType.DMA((NREMOTE,)),
            pltpu.SemaphoreType.DMA((NLOCAL,)),
        ],
        compiler_params=pltpu.CompilerParams(
            collective_id=0, has_side_effects=True, vmem_limit_bytes=60 * 1024 * 1024
        ),
    )(
        hidden.reshape(32, D),
        gain,
        above.reshape(32, D),
        kc.reshape(TOK, 128),
        vc.reshape(TOK, 128),
        wk.reshape(4, 4, 512, 128),
        wv.reshape(4, 4, 512, 128),
        ak.reshape(1024, 128),
        av.reshape(1024, 128),
        mk.reshape(1024, 128),
        mv.reshape(1024, 128),
    )
    return tuple(o[None] for o in outs[:4]) + (outs[4][None, None],)


def solution(mesh):
    square = P("section", "island", "tensor")
    wide = P("island", "section", None, "tensor")
    return jax.shard_map(
        local,
        mesh=mesh,
        in_specs=(
            P("island", "section", "tensor", None),
            P("section", None),
            P("island", "tensor", None),
            wide,
            wide,
            wide,
            wide,
            square,
            square,
            square,
            square,
        ),
        out_specs=(square, square, square, square, P("island", "section", "tensor", None)),
        check_vma=False,
    )
```

time: 239 us -> 99.2 us (0.42)
  waiting for transfers between devices: 191 us -> 0 us
  Pallas kernels: 0 us -> 91.2 us
  matrix products: 16 us -> 0 us
  between operations: 13.9 us -> 0.67 us
  other arithmetic: 11.3 us -> 0 us
  local copies, waits for them, and re-layouts: 0.72 us -> 6.24 us
  starting transfers between devices: 4.16 us -> 0 us
    pallas_call x0 -> x1, Pallas kernels: none -> 91.2 us  [local(): pl.pallas_call(kernel, out_shape=[jax.ShapeDtypeStruct((1024, 128), F32)]...]
    ppermute x3 -> x0, waiting for transfers between devices: 74.1 us -> none  [from_behind(): return lax.ppermute(block, axis, route)]
    reduce_scatter x3 -> x0, waiting for transfers between devices: 63.1 us -> none  [the longest x1 58.8 us: local(): lax.psum_scatter(((contract_cols(key_piece, weight_key) + contract_cols(v...]
    all_gather x1 -> x0, waiting for transfers between devices: 53.9 us -> none  [local(): piece = lax.all_gather(normed, 'tensor', axis=0, tiled=True)]
    dot_general x4 -> x0, matrix products: 16 us -> none  [the longest x2 9.69 us: contract_rows(): lax.dot_general(left, right, (((0,), (0,)), ((), ())), preferred_element_...]
    unnamed x20 -> x11, local copies, waits for them, and re-layouts: 0.72 us -> 6.24 us
    broadcast_in_dim x3 -> x0, other arithmetic: 5.02 us -> none  [the longest x1 2.07 us: local(): momentum_value_new[None]]
    convert_element_type x3 -> x0, other arithmetic: 4.83 us -> none  [local(): running.astype(jnp.bfloat16)]
  transfers between devices with their start and end apart: 7 -> 0, of which waited for: 6 -> 0; matrix products, arithmetic and copies ran while one was open for 4% -> 0% of each run, Pallas kernels for 0% -> 0%
where the time goes in v1:
time: 99.2 us; the launch traced here: 98.1 us
  Pallas kernels  91.2 us (92%)
  local copies, waits for them, and re-layouts  6.24 us (6%)
    pallas_call x1, Pallas kernels, local(): pl.pallas_call(kernel, out_shape=[jax.ShapeDtypeStruct((1024, 128), F32)]...  91.2 us
    unnamed x11, local copies, waits for them, and re-layouts  6.24 us

profile of v1, /device:TPU:1, one launch (start us, length us, event | category | flops | bytes accessed | tf_op | source)
XLA Modules:
  0.0 98.1 jit_solution(964607692095425788)
XLA Ops:
  0.6 91.2 %shard_map.146 = (f32[1024,128]{1,0:T(8,128)}, f32[1024,128]{1,0:T(8,128)}, f32[1024,128]{1,0:T(8,128)}, f32[1024,128]{1,0:T(8,128)}, bf16[32,8192]{1,0:T(8,128)(2,1)}) custom-call(bf16[32,8192]{1,0:T(8,128)(2,1)} %bitcast.17, bf16[1,8192]{1,0:T(2,128)(2,1)} %refs_1_.1, bf16[32,8192]{1,0:T(8,128)(2,1)} %bitcast.18, bf16[256,128]{1,0:T(8,128)(2,1)} %bitcast.28, ...), custom_call_target="tpu_custom_call" | custom-call | tf_op jit(solution)/shard_map/pallas_call | solution.py:592
  91.8 0.0 copy-start.2
  91.8 0.0 copy-start.1
  91.8 0.0 copy-start
  91.8 2.0 %copy.21 = f32[1,1024,128]{2,1,0:T(8,128)} copy(f32[1,1024,128]{2,1,0:T(8,128)} %bitcast.27) | data formatting | bytes 1048576
  93.8 1.9 %copy.22 = f32[1,1024,128]{2,1,0:T(8,128)} copy(f32[1,1024,128]{2,1,0:T(8,128)} %bitcast.26) | data formatting | bytes 1048576
  95.7 0.0 copy-done.2
  95.7 0.8 copy.23
  96.5 0.0 copy-done.1
  96.5 0.8 copy.24
  97.3 0.0 copy-done
  97.3 0.8 copy.25
Async XLA Ops:
  91.8 3.9 %copy-start.2 = (f32[1024,128]{1,0:T(8,128)S(1)}, f32[1024,128]{1,0:T(8,128)}, u32[]{:S(2)}) copy-start(f32[1024,128]{1,0:T(8,128)} %get-tuple-element.12) | copy-start | bytes 1572868
  91.8 4.7 %copy-start.1 = (f32[1024,128]{1,0:T(8,128)S(1)}, f32[1024,128]{1,0:T(8,128)}, u32[]{:S(2)}) copy-start(f32[1024,128]{1,0:T(8,128)} %get-tuple-element.13) | copy-start | bytes 1572868
  91.8 5.5 %copy-start = (bf16[32,8192]{1,0:T(8,128)(2,1)S(1)}, bf16[32,8192]{1,0:T(8,128)(2,1)}, u32[]{:S(2)}) copy-start(bf16[32,8192]{1,0:T(8,128)(2,1)} %get-tuple-element.14) | copy-start | bytes 1572868
